TPU v7x, 512 devices: a 8x2x16 block of a 8x8x16 slice. The times are simulated.
512 devices in a mesh: grp: 2 (over y), sp: 16 (over z), blk: 8 (over x), rep: 2 (over core).
Axes of the slice: x: 8, y: 2, z: 16, core: 2. Of those that a mesh axis runs over, the one named last changes fastest.
The devices are a block of a 8x8x16 slice.
Arguments:
- hidden: bfloat16 [16, 2048, 4096], P(('grp', 'blk'), 'sp'), parts along dimension 0, may hold values from -64 to 64
- queries: bfloat16 [16, 2048, 4096], P(('grp', 'blk'), 'sp', 'rep'), parts along dimension 0, may hold values from -600 to 600
- norm_gain: float32 [4096], replicated, may hold values from 0.1 to 1.9
- key_matrix: bfloat16 [4096, 1024], P('sp', 'rep'), may hold values from -0.09375 to 0.09375
- value_matrix: bfloat16 [4096, 1024], P('sp', 'rep'), may hold values from -0.09375 to 0.09375
- key_shift_bias: bfloat16 [1024], P('rep'), may hold values from -3 to 3
- value_shift_bias: bfloat16 [1024], P('rep'), may hold values from -3 to 3
- doc_lengths: int32 [16], P('grp'), parts along dimension 0, may hold values from 1 to 4097, 16384 in all
Outputs:
- attended: bfloat16 [16, 2048, 4096], P(('grp', 'blk'), 'sp', 'rep'), parts along dimension 0
There are 2 independent parts, one for each index of `grp`. A program takes and returns all parts, laid end to end along the dimension named above; an argument that names none is the same for every part. Nothing has to cross between parts.
Inputs may be any that keep to these rules, and one draw needn't show every extreme that they name: `doc_lengths`: the lengths of the 8 documents packed in order into the sequence; they sum to 16384, and the longest is exactly 4097 tokens.
All inputs are finite; a program needn't handle non-finite values.
Results may differ from a plain program's by a relative error of at most 0.012.
The roundings to bfloat16 on the way count: a program that leaves them out, or rounds other values in their place, can miss the bound.
Values may be sent and summed in bfloat16 or wider, within the bound.
A program may use at most 64 MiB of HBM per device.

v0:
```python
import math

import jax
import jax.numpy as jnp
from jax import lax
from jax.sharding import PartitionSpec as P

HEAD_DIMENSION = 128


EPS_VALUE = 1e-06
THETA_BASE = 1000000.0
NEG_FILL = -1e30


def in_one_piece(arrays, axis, dim, along):
    widths = [a.shape[along] for a in arrays]
    both = jnp.concatenate(arrays, axis=along)
    result = lax.all_gather(both, axis, axis=dim, tiled=True)
    return tuple(jnp.split(result, [sum(widths[:k]) for k in range(1, len(widths))], axis=along))


def in_one_piece_2(arrays, axis, split_dim, concat_dim, along):
    widths = [a.shape[along] for a in arrays]
    both = jnp.concatenate(arrays, axis=along)
    result = lax.all_to_all(both, axis, split_axis=split_dim, concat_axis=concat_dim, tiled=True)
    return tuple(jnp.split(result, [sum(widths[:k]) for k in range(1, len(widths))], axis=along))


def shifted(block, axis, distance):
    devices = range(lax.axis_size(axis))
    route = [(i - distance, i) for i in devices if i - distance in devices]
    return lax.ppermute(block, axis, route)


def in_blocks(value, dim, size):
    shape = value.shape
    pieces = value.reshape(*shape[:dim], size, shape[dim] // size, *shape[dim + 1 :])
    return jnp.moveaxis(pieces, dim, 0)


def edges_of(length, count):
    unit = 8 if length >= 8 * count else 1
    return [length // unit * k // count * unit for k in range(1, count)]


def laid_out(pieces, dim):
    shape = list(pieces.shape[1:])
    shape[dim] *= pieces.shape[0]
    return jnp.moveaxis(pieces, 0, dim).reshape(shape)


def exchange_in_pieces(value, axis, pieces, split_dim, concat_dim):
    blocks = in_blocks(value, split_dim, lax.axis_size(axis))
    widest = max(range(1, max(2, blocks.ndim - 1)), key=lambda d: blocks.shape[d])
    gathered = []
    for share in jnp.split(blocks, edges_of(blocks.shape[widest], pieces), axis=widest):
        if share.size:
            gathered.append(lax.all_to_all(share, axis, split_axis=0, concat_axis=0, tiled=True))
    return laid_out(jnp.concatenate(gathered, axis=widest), concat_dim)


def apply_rotation(projected, token_places):
    half_size = projected.shape[-1] // 2
    freq_index = jnp.arange(half_size).astype(jnp.float32)
    inverse = jnp.exp(freq_index * (-2.0 * math.log(THETA_BASE) / projected.shape[-1]))
    angles = token_places[:, None] * inverse[None, :]
    cosine = jnp.cos(angles)[:, None, :]
    sine = jnp.sin(angles)[:, None, :]
    first_half = projected[..., :half_size]
    second_half = projected[..., half_size:]
    return jnp.concatenate(
        [first_half * cosine - second_half * sine, second_half * cosine + first_half * sine],
        axis=-1,
    )


def doc_index(token_places, doc_lengths):
    ending = jnp.cumsum(doc_lengths)
    return jnp.sum((token_places[:, None] >= ending[None, :]).astype(jnp.int32), axis=1)


def on_device(
    hidden,
    queries,
    norm_gain,
    key_matrix,
    value_matrix,
    key_shift_bias,
    value_shift_bias,
    doc_lengths,
):
    sp_count = lax.axis_size("sp")
    sp_place = lax.axis_index("sp")
    cycle_place = lax.axis_index("blk")
    local_rows = hidden.shape[1]
    span_rows = local_rows * sp_count
    head_size = HEAD_DIMENSION
    kv_local = key_matrix.shape[1] // head_size
    fold_count = sp_count // kv_local
    rows_all = hidden[0].astype(jnp.float32)
    row_scale = lax.rsqrt(jnp.mean(rows_all * rows_all, axis=1, keepdims=True) + EPS_VALUE)
    normed = (rows_all * row_scale * norm_gain).astype(jnp.bfloat16)
    span_places = cycle_place * span_rows + jnp.arange(span_rows)
    weight_pieces = in_one_piece((key_matrix, value_matrix), "sp", 0, 1)
    key_projector = jnp.dot(normed, weight_pieces[0], preferred_element_type=jnp.float32)
    value_projector = jnp.dot(normed, weight_pieces[1], preferred_element_type=jnp.float32)
    local_places = cycle_place * span_rows + sp_place * local_rows + jnp.arange(local_rows)
    key_projector = key_projector + key_shift_bias.astype(jnp.float32)
    value_projector = value_projector + value_shift_bias.astype(jnp.float32)
    keys_local = apply_rotation(
        key_projector.reshape(local_rows, kv_local, head_size), local_places.astype(jnp.float32)
    ).astype(jnp.bfloat16)
    values_local = value_projector.reshape(local_rows, kv_local, head_size).astype(jnp.bfloat16)
    keys_copies = jnp.repeat(keys_local, fold_count, axis=1).reshape(
        1, local_rows, sp_count * head_size
    )
    values_copies = jnp.repeat(values_local, fold_count, axis=1).reshape(
        1, local_rows, sp_count * head_size
    )
    query_span, keys_span, values_span = in_one_piece_2(
        (queries, keys_copies, values_copies), "sp", 2, 1, 0
    )
    keys_span = keys_span[0]
    values_span = values_span[0]
    heads_here = query_span.shape[2] // head_size
    query_heads = query_span[0].reshape(span_rows, heads_here, head_size)
    query_docs = doc_index(span_places, doc_lengths)
    scale_factor = 1.0 / math.sqrt(head_size)

    def absorb(carry, kv_pieces, offset):
        key_piece, value_piece = kv_pieces
        piece_rows = key_piece.shape[0]
        block_rows = 512

        def block_step(block_number, state):
            block_start = block_number * block_rows
            key_block = lax.dynamic_slice_in_dim(key_piece, block_start, block_rows, 0)
            value_block = lax.dynamic_slice_in_dim(value_piece, block_start, block_rows, 0)
            key_places = offset + block_start + jnp.arange(block_rows)
            key_docs = doc_index(key_places, doc_lengths)

            def update(inner):
                running_max, running_total, running_sum = inner
                scores = (
                    jnp.einsum(
                        "qhd,kd->hqk", query_heads, key_block, preferred_element_type=jnp.float32
                    )
                    * scale_factor
                )
                visible = (
                    (key_places[None, :] <= span_places[:, None])
                    & (key_docs[None, :] == query_docs[:, None])
                    & (key_places[None, :] >= 0)
                )
                scores = jnp.where(visible[None], scores, NEG_FILL)
                new_max = jnp.maximum(running_max, jnp.max(scores, axis=2))
                weights = jnp.where(
                    visible[None], jnp.exp(scores - new_max[..., None]), 0.0
                ).astype(jnp.bfloat16)
                factor = jnp.exp(running_max - new_max)
                new_total = factor * running_total + jnp.sum(weights.astype(jnp.float32), axis=2)
                new_sum = factor[..., None] * running_sum + jnp.einsum(
                    "hqk,kd->hqd", weights, value_block, preferred_element_type=jnp.float32
                )
                return (new_max, new_total, new_sum)

            reachable = (
                (offset + block_start + block_rows > 0)
                & (offset + block_start <= span_places[-1])
                & (key_docs[-1] >= query_docs[0])
            )
            return lax.cond(reachable, update, lambda inner: inner, state)

        return lax.fori_loop(0, piece_rows // block_rows, block_step, carry)

    start_state = (
        jnp.full((heads_here, span_rows), NEG_FILL, jnp.float32),
        jnp.zeros((heads_here, span_rows), jnp.float32),
        jnp.zeros((heads_here, span_rows, head_size), jnp.float32),
    )
    state_now = absorb(start_state, (keys_span, values_span), cycle_place * span_rows)
    for back_count in (1, 2):
        earlier_keys, earlier_values = shifted((keys_span, values_span), "blk", back_count)
        state_now = absorb(
            state_now, (earlier_keys, earlier_values), (cycle_place - back_count) * span_rows
        )
    final_max, final_total, final_sum = state_now
    result = (final_sum / final_total[..., None]).astype(jnp.bfloat16)
    result = result.transpose(1, 0, 2).reshape(1, span_rows, heads_here * head_size)
    return exchange_in_pieces(result, "sp", 2, 1, 2)


def solution(mesh):
    in_specs = (
        P(("grp", "blk"), "sp", None),
        P(("grp", "blk"), "sp", "rep"),
        P(),
        P("sp", "rep"),
        P("sp", "rep"),
        P("rep"),
        P("rep"),
        P("grp"),
    )
    out_specs = P(("grp", "blk"), "sp", "rep")
    return jax.shard_map(
        on_device, mesh=mesh, in_specs=in_specs, out_specs=out_specs, check_vma=False
    )
```

profile of v0, /device:TPU:88, one launch (start us, length us, event | category | flops | bytes accessed | tf_op | source)
XLA Modules:
  0.0 467.6 jit_solution(7173407353085068850)
XLA Ops:
  13.1 136.9 %all-gather.2.cloned.1.call-done = bf16[4096,1024]{1,0:T(8,128)(2,1)} async-done(((bf16[256,1024]{1,0:T(8,128)(2,1)}), bf16[4096,1024]{1,0:T(8,128)(2,1)}) %all-gather.2.cloned.1.call-update) | async-done | bytes 8388624 | tf_op jit(solution)/shard_map/all_gather | solution.py:19
  149.9 3.3 fusion.34
  154.0 3.0 fusion.40
  157.5 10.8 %copy.49 = bf16[3,128,2048]{1,0,2:T(4,128)(2,1)} copy(bf16[3,128,2048]{1,2,0:T(8,128)(2,1)S(1)} %pad_maximum_fusion) | data formatting | bytes 3145728 | tf_op jit(solution)/shard_map/concatenate | solution.py:25
  168.3 8.6 %all-to-all-start = ((bf16[3,128,2048]{1,0,2:T(4,128)(2,1)}), bf16[3,128,2048]{1,0,2:T(4,128)(2,1)S(1)}, u32[]{:S(2)}, u32[]{:S(2)}) async-start(bf16[3,128,2048]{1,0,2:T(4,128)(2,1)} %copy.49), calls=%async_computation | async-start | bytes 4194304 | tf_op jit(solution)/shard_map/all_to_all | solution.py:26
  177.2 95.0 %all-to-all-done = bf16[3,128,2048]{1,0,2:T(4,128)(2,1)S(1)} async-done(((bf16[3,128,2048]{1,0,2:T(4,128)(2,1)}), bf16[3,128,2048]{1,0,2:T(4,128)(2,1)S(1)}, u32[]{:S(2)}, u32[]{:S(2)}) %all-to-all-start) | async-done | bytes 1572896 | tf_op jit(solution)/shard_map/all_to_all | solution.py:26
  273.6 2.6 collective-permute-start
  276.2 2.5 collective-permute-start.2
  281.7 2.1 collective-permute-start.3
  284.2 47.5 %while.57 = (s32[]{:T(128)}, f32[1,2048]{1,0:T(1,128)S(1)}, f32[1,2048]{1,0:T(1,128)S(1)}, f32[1,2048,128]{2,1,0:T(8,128)S(1)}, s32[]{:T(128)}, /*index=5*/s32[2...) while((s32[]{:T(128)}, f32[1,2048]{1,0:T(1,128)S(1)}, ...), condition=%wide.region_9.10_spmd, body=%wide.region_3.9_spmd.sunk | while | flops 565724160 | bytes 15673809 | solution.py:175
  288.1 8.0 %conditional.6 = ((f32[1,2048]{1,0:T(1,128)S(1)}, f32[1,2048]{1,0:T(1,128)S(1)}, f32[1,2048,128]{2,1,0:T(8,128)S(1)})) conditional(s32[]{:T(128)} %convert_element_type.183, (f32[1,2048]{1,0:T(1,128)S(1)}, f32[1,2048]{1,0:T(1,128)S(1)}, f32[1,2048,128]{2,1,0:T(8,128)S(1)}) %tuple.158, (s32[]{:T(128)}, s32[512]{0:T(512)S(1)}, s32[2048]{0:T(1024)S(1)}, ...), branch_computations={%region_5.5_spmd, %region_6.8_spmd} | conditional | flops 565711872 | bytes 15665230 | solution.py:173
  288.1 2.5 fusion
  290.7 2.1 convert_reduce_fusion
  292.8 3.2 fusion.1
  300.0 8.0 %conditional.6 = ((f32[1,2048]{1,0:T(1,128)S(1)}, f32[1,2048]{1,0:T(1,128)S(1)}, f32[1,2048,128]{2,1,0:T(8,128)S(1)})) conditional(s32[]{:T(128)} %convert_element_type.183, (f32[1,2048]{1,0:T(1,128)S(1)}, f32[1,2048]{1,0:T(1,128)S(1)}, f32[1,2048,128]{2,1,0:T(8,128)S(1)}) %tuple.158, (s32[]{:T(128)}, s32[512]{0:T(512)S(1)}, s32[2048]{0:T(1024)S(1)}, ...), branch_computations={%region_5.5_spmd, %region_6.8_spmd} | conditional | flops 565711872 | bytes 15665230 | solution.py:173
  300.0 2.5 fusion
  302.6 2.1 convert_reduce_fusion
  304.7 3.2 fusion.1
  311.8 8.0 %conditional.6 = ((f32[1,2048]{1,0:T(1,128)S(1)}, f32[1,2048]{1,0:T(1,128)S(1)}, f32[1,2048,128]{2,1,0:T(8,128)S(1)})) conditional(s32[]{:T(128)} %convert_element_type.183, (f32[1,2048]{1,0:T(1,128)S(1)}, f32[1,2048]{1,0:T(1,128)S(1)}, f32[1,2048,128]{2,1,0:T(8,128)S(1)}) %tuple.158, (s32[]{:T(128)}, s32[512]{0:T(512)S(1)}, s32[2048]{0:T(1024)S(1)}, ...), branch_computations={%region_5.5_spmd, %region_6.8_spmd} | conditional | flops 565711872 | bytes 15665230 | solution.py:173
  311.9 2.5 fusion
  314.5 2.1 convert_reduce_fusion
  316.6 3.2 fusion.1
  323.7 8.0 %conditional.6 = ((f32[1,2048]{1,0:T(1,128)S(1)}, f32[1,2048]{1,0:T(1,128)S(1)}, f32[1,2048,128]{2,1,0:T(8,128)S(1)})) conditional(s32[]{:T(128)} %convert_element_type.183, (f32[1,2048]{1,0:T(1,128)S(1)}, f32[1,2048]{1,0:T(1,128)S(1)}, f32[1,2048,128]{2,1,0:T(8,128)S(1)}) %tuple.158, (s32[]{:T(128)}, s32[512]{0:T(512)S(1)}, s32[2048]{0:T(1024)S(1)}, ...), branch_computations={%region_5.5_spmd, %region_6.8_spmd} | conditional | flops 565711872 | bytes 15665230 | solution.py:173
  323.8 2.5 fusion
  326.3 2.1 convert_reduce_fusion
  328.5 3.2 fusion.1
  331.8 4.8 %collective-permute-done.1 = bf16[2048,128]{1,0:T(8,128)(2,1)} collective-permute-done((bf16[2048,128]{1,0:T(8,128)(2,1)}, bf16[2048,128]{1,0:T(8,128)(2,1)}, u32[]{:S(2)}, u32[]{:S(2)}) %collective-permute-start.1) | collective-permute-done | bytes 524320 | tf_op jit(solution)/shard_map/ppermute | solution.py:33
  336.6 43.2 %while.58 = (s32[]{:T(128)}, f32[1,2048]{1,0:T(1,128)S(1)}, f32[1,2048]{1,0:T(1,128)S(1)}, f32[1,2048,128]{2,1,0:T(8,128)S(1)}, s32[]{:T(128)}, /*index=5*/s32[2...) while((s32[]{:T(128)}, f32[1,2048]{1,0:T(1,128)S(1)}, ...), condition=%wide.region_16.17_spmd, body=%wide.region_10.16_spmd.sunk | while | flops 565724160 | bytes 15673809 | solution.py:175
  340.4 7.0 %conditional.7 = ((f32[1,2048]{1,0:T(1,128)S(1)}, f32[1,2048]{1,0:T(1,128)S(1)}, f32[1,2048,128]{2,1,0:T(8,128)S(1)})) conditional(s32[]{:T(128)} %convert_element_type.185, (f32[1,2048]{1,0:T(1,128)S(1)}, f32[1,2048]{1,0:T(1,128)S(1)}, f32[1,2048,128]{2,1,0:T(8,128)S(1)}) %tuple.161, (s32[]{:T(128)}, s32[512]{0:T(512)S(1)}, s32[2048]{0:T(1024)S(1)}, ...), branch_computations={%region_12.12_spmd, %region_13.15_spmd} | conditional | flops 565711872 | bytes 15665230 | solution.py:173
  341.9 2.1 convert_reduce_fusion.2
  344.1 3.2 fusion.10
  351.2 7.0 %conditional.7 = ((f32[1,2048]{1,0:T(1,128)S(1)}, f32[1,2048]{1,0:T(1,128)S(1)}, f32[1,2048,128]{2,1,0:T(8,128)S(1)})) conditional(s32[]{:T(128)} %convert_element_type.185, (f32[1,2048]{1,0:T(1,128)S(1)}, f32[1,2048]{1,0:T(1,128)S(1)}, f32[1,2048,128]{2,1,0:T(8,128)S(1)}) %tuple.161, (s32[]{:T(128)}, s32[512]{0:T(512)S(1)}, s32[2048]{0:T(1024)S(1)}, ...), branch_computations={%region_12.12_spmd, %region_13.15_spmd} | conditional | flops 565711872 | bytes 15665230 | solution.py:173
  352.7 2.1 convert_reduce_fusion.2
  354.9 3.2 fusion.10
  362.0 6.9 %conditional.7 = ((f32[1,2048]{1,0:T(1,128)S(1)}, f32[1,2048]{1,0:T(1,128)S(1)}, f32[1,2048,128]{2,1,0:T(8,128)S(1)})) conditional(s32[]{:T(128)} %convert_element_type.185, (f32[1,2048]{1,0:T(1,128)S(1)}, f32[1,2048]{1,0:T(1,128)S(1)}, f32[1,2048,128]{2,1,0:T(8,128)S(1)}) %tuple.161, (s32[]{:T(128)}, s32[512]{0:T(512)S(1)}, s32[2048]{0:T(1024)S(1)}, ...), branch_computations={%region_12.12_spmd, %region_13.15_spmd} | conditional | flops 565711872 | bytes 15665230 | solution.py:173
  365.7 3.2 fusion.10
  372.8 7.0 %conditional.7 = ((f32[1,2048]{1,0:T(1,128)S(1)}, f32[1,2048]{1,0:T(1,128)S(1)}, f32[1,2048,128]{2,1,0:T(8,128)S(1)})) conditional(s32[]{:T(128)} %convert_element_type.185, (f32[1,2048]{1,0:T(1,128)S(1)}, f32[1,2048]{1,0:T(1,128)S(1)}, f32[1,2048,128]{2,1,0:T(8,128)S(1)}) %tuple.161, (s32[]{:T(128)}, s32[512]{0:T(512)S(1)}, s32[2048]{0:T(1024)S(1)}, ...), branch_computations={%region_12.12_spmd, %region_13.15_spmd} | conditional | flops 565711872 | bytes 15665230 | solution.py:173
  376.5 3.2 fusion.10
  379.8 32.9 %while.59 = (s32[]{:T(128)}, f32[1,2048]{1,0:T(1,128)S(1)}, f32[1,2048]{1,0:T(1,128)S(1)}, f32[1,2048,128]{2,1,0:T(8,128)S(1)}, s32[]{:T(128)}, /*index=5*/s32[2...) while((s32[]{:T(128)}, f32[1,2048]{1,0:T(1,128)S(1)}, ...), condition=%wide.region_23.24_spmd, body=%wide.region_17.23_spmd.sunk | while | flops 565724160 | bytes 15673809 | solution.py:175
  387.3 6.0 %conditional.8 = ((f32[1,2048]{1,0:T(1,128)S(1)}, f32[1,2048]{1,0:T(1,128)S(1)}, f32[1,2048,128]{2,1,0:T(8,128)S(1)})) conditional(s32[]{:T(128)} %convert_element_type.187, (f32[1,2048]{1,0:T(1,128)S(1)}, f32[1,2048]{1,0:T(1,128)S(1)}, f32[1,2048,128]{2,1,0:T(8,128)S(1)}) %tuple.164, (s32[]{:T(128)}, s32[512]{0:T(512)S(1)}, s32[2048]{0:T(1024)S(1)}, ...), branch_computations={%region_19.19_spmd, %region_20.22_spmd} | conditional | flops 565711872 | bytes 15665230 | solution.py:173
  391.0 2.3 fusion.19
  396.9 6.1 %conditional.8 = ((f32[1,2048]{1,0:T(1,128)S(1)}, f32[1,2048]{1,0:T(1,128)S(1)}, f32[1,2048,128]{2,1,0:T(8,128)S(1)})) conditional(s32[]{:T(128)} %convert_element_type.187, (f32[1,2048]{1,0:T(1,128)S(1)}, f32[1,2048]{1,0:T(1,128)S(1)}, f32[1,2048,128]{2,1,0:T(8,128)S(1)}) %tuple.164, (s32[]{:T(128)}, s32[512]{0:T(512)S(1)}, s32[2048]{0:T(1024)S(1)}, ...), branch_computations={%region_19.19_spmd, %region_20.22_spmd} | conditional | flops 565711872 | bytes 15665230 | solution.py:173
  400.6 2.4 fusion.19
  406.6 6.0 %conditional.8 = ((f32[1,2048]{1,0:T(1,128)S(1)}, f32[1,2048]{1,0:T(1,128)S(1)}, f32[1,2048,128]{2,1,0:T(8,128)S(1)})) conditional(s32[]{:T(128)} %convert_element_type.187, (f32[1,2048]{1,0:T(1,128)S(1)}, f32[1,2048]{1,0:T(1,128)S(1)}, f32[1,2048,128]{2,1,0:T(8,128)S(1)}) %tuple.164, (s32[]{:T(128)}, s32[512]{0:T(512)S(1)}, s32[2048]{0:T(1024)S(1)}, ...), branch_computations={%region_19.19_spmd, %region_20.22_spmd} | conditional | flops 565711872 | bytes 15665230 | solution.py:173
  410.3 2.3 fusion.19
  413.8 23.4 %all_to_all.25 = bf16[16,1,64,128]{3,2,1,0:T(8,128)(2,1)S(1)} all-to-all(bf16[16,1,64,128]{3,2,1,0:T(8,128)(2,1)S(1)} %get-tuple-element.1326), channel_id=1, replica_groups=mesh['grp'=2,'sp'=16,'blk'=8,'rep'=2] {'sp'}, dimensions={0} | all-to-all | bytes 524288 | tf_op jit(solution)/shard_map/all_to_all | solution.py:59
  437.2 5.7 %all-to-all-start.2 = ((bf16[16,1,64,128]{3,2,1,0:T(8,128)(2,1)}), bf16[16,1,64,128]{3,2,1,0:T(8,128)(2,1)S(1)}, u32[]{:S(2)}, u32[]{:S(2)}) async-start(bf16[16,1,64,128]{3,2,1,0:T(8,128)(2,1)} %get-tuple-element.1327), calls=%async_computation.2 | async-start | bytes 524288 | tf_op jit(solution)/shard_map/all_to_all | solution.py:59
  443.2 15.9 %all-to-all-done.2 = bf16[16,1,64,128]{3,2,1,0:T(8,128)(2,1)S(1)} async-done(((bf16[16,1,64,128]{3,2,1,0:T(8,128)(2,1)}), bf16[16,1,64,128]{3,2,1,0:T(8,128)(2,1)S(1)}, u32[]{:S(2)}, u32[]{:S(2)}) %all-to-all-start.2) | async-done | bytes 262176 | tf_op jit(solution)/shard_map/all_to_all | solution.py:59
  (175 shorter events, 59.4 us)
Async XLA Ops:
  6.5 143.4 %all-gather.2.cloned.1.call-start = ((), (), s32[]{:S(2)}) async-start(), calls=%async_computation.3 | async-start | bytes 8912896 | tf_op jit(solution)/shard_map/all_gather | solution.py:19
  13.1 140.9 %copy-start = (bf16[1,128,4096]{2,1,0:T(8,128)(2,1)S(1)}, bf16[1,128,4096]{2,1,0:T(8,128)(2,1)}, u32[]{:S(2)}) copy-start(bf16[1,128,4096]{2,1,0:T(8,128)(2,1)} %param.20) | copy-start | bytes 3145732
  13.1 140.9 %copy-start.1 = (f32[4096]{0:T(1024)S(1)}, f32[4096]{0:T(1024)}, u32[]{:S(2)}) copy-start(f32[4096]{0:T(1024)} %param.22) | copy-start | bytes 49156
  157.5 19.4 %copy-start.2 = (s32[8]{0:T(128)S(1)}, s32[8]{0:T(128)}, u32[]{:S(2)}) copy-start(s32[8]{0:T(128)} %param.27) | copy-start | bytes 100
  168.3 104.0 %all-to-all-start = ((bf16[3,128,2048]{1,0,2:T(4,128)(2,1)}), bf16[3,128,2048]{1,0,2:T(4,128)(2,1)S(1)}, u32[]{:S(2)}, u32[]{:S(2)}) async-start(bf16[3,128,2048]{1,0,2:T(4,128)(2,1)} %copy.49), calls=%async_computation | async-start | bytes 4194304 | tf_op jit(solution)/shard_map/all_to_all | solution.py:26
  273.6 58.2 %collective-permute-start = (bf16[2048,128]{1,0:T(8,128)(2,1)}, bf16[2048,128]{1,0:T(8,128)(2,1)S(1)}, u32[]{:S(2)}, u32[]{:S(2)}) collective-permute-start(bf16[2048,128]{1,0:T(8,128)(2,1)} %bitcast.45), channel_id=1, source_target_pairs={{0,2},{2,4},{4,6},{6,8},{8,10},{10,12},{12,14},{1,3},{3,5},{5,7},{... | collective-permute-start | bytes 1572872 | tf_op jit(solution)/shard_map/ppermute | solution.py:33
  276.2 103.5 %collective-permute-start.2 = (bf16[2048,128]{1,0:T(8,128)(2,1)}, bf16[2048,128]{1,0:T(8,128)(2,1)S(1)}, u32[]{:S(2)}, u32[]{:S(2)}) collective-permute-start(bf16[2048,128]{1,0:T(8,128)(2,1)} %bitcast.45), channel_id=1, source_target_pairs={{0,4},{2,6},{4,8},{6,10},{8,12},{10,14},{1,5},{3,7},{5,9},{7,11},{... | collective-permute-start | bytes 1572872 | tf_op jit(solution)/shard_map/ppermute | solution.py:33
  279.8 56.8 %collective-permute-start.1 = (bf16[2048,128]{1,0:T(8,128)(2,1)}, bf16[2048,128]{1,0:T(8,128)(2,1)}, u32[]{:S(2)}, u32[]{:S(2)}) collective-permute-start(bf16[2048,128]{1,0:T(8,128)(2,1)} %bitcast.48), channel_id=1, source_target_pairs={{0,2},{2,4},{4,6},{6,8},{8,10},{10,12},{12,14},{1,3},{3,5},{5,7},{... | collective-permute-start | bytes 1572872 | tf_op jit(solution)/shard_map/ppermute | solution.py:33
  281.7 98.1 %collective-permute-start.3 = (bf16[2048,128]{1,0:T(8,128)(2,1)}, bf16[2048,128]{1,0:T(8,128)(2,1)S(1)}, u32[]{:S(2)}, u32[]{:S(2)}) collective-permute-start(bf16[2048,128]{1,0:T(8,128)(2,1)} %bitcast.48), channel_id=1, source_target_pairs={{0,4},{2,6},{4,8},{6,10},{8,12},{10,14},{1,5},{3,7},{5,9},{7,11},{... | collective-permute-start | bytes 1572872 | tf_op jit(solution)/shard_map/ppermute | solution.py:33
  437.2 22.0 %all-to-all-start.2 = ((bf16[16,1,64,128]{3,2,1,0:T(8,128)(2,1)}), bf16[16,1,64,128]{3,2,1,0:T(8,128)(2,1)S(1)}, u32[]{:S(2)}, u32[]{:S(2)}) async-start(bf16[16,1,64,128]{3,2,1,0:T(8,128)(2,1)} %get-tuple-element.1327), calls=%async_computation.2 | async-start | bytes 524288 | tf_op jit(solution)/shard_map/all_to_all | solution.py:59
Sparse Core Ops, SparseCore 0:
  9.4 140.4 all-gather.1
where the time goes:
time: 468 us
  waiting for transfers between devices  253 us (54%)
  matrix products  59.6 us (13%)
  local copies, waits for them, and re-layouts  39 us (8%)
  other arithmetic  31.8 us (7%)
  loops' own time  23.8 us (5%)
  starting transfers between devices  23.6 us (5%)
  blocking collectives  23.4 us (5%)
  between operations  13.7 us (3%)
    all_gather x1, waiting for transfers between devices, in_one_piece(): result = lax.all_gather(both, axis, axis=dim, tiled=True)  137 us
    all_to_all x1, waiting for transfers between devices, in_one_piece_2(): lax.all_to_all(both, axis, split_axis=split_dim, concat_axis=concat_dim,...  95 us
    dot_general x11, matrix products, update(): jnp.einsum('hqk,kd->hqd', weights, value_block, preferred_element_type=jn...  33 us
    reduce_sum x11, other arithmetic, update(): jnp.sum(weights.astype(jnp.float32), axis=2)  23.4 us
    all_to_all x1, blocking collectives, exchange_in_pieces(): lax.all_to_all(share, axis, split_axis=0, concat_axis=0, tiled=True)  23.4 us
    another operation x3, loops' own time, absorb(): return lax.fori_loop(0, piece_rows // block_rows, block_step, carry)  23.1 us
    dot_general x11, matrix products, update(): jnp.einsum('qhd,kd->hqk', query_heads, key_block, preferred_element_type=...  20.3 us
    all_to_all x1, waiting for transfers between devices, exchange_in_pieces(): lax.all_to_all(share, axis, split_axis=0, concat_axis=0, tiled=True)  15.9 us
  transfers between devices with their start and end apart: 7, of which 4 were waited for; matrix products, arithmetic and copies ran while one was open for 17% of the time, Pallas kernels for 0%

commit v1 on v0

v1 whole, which is shorter than its diff:
```python
import functools
import math

import jax
import jax.numpy as jnp
from jax import lax
from jax.experimental import pallas as pl
from jax.experimental.pallas import tpu as pltpu
from jax.sharding import PartitionSpec as P

HEAD = 128
EPS_VALUE = 1e-06
THETA_BASE = 1000000.0
NEG_FILL = -1e30
TILE = 512
MESH = pl.DeviceIdType.MESH
F32 = jnp.float32
BF16 = jnp.bfloat16


def ring_offsets(n):
    order = [0]
    for k in range(1, n // 2):
        order += [-k, k]
    return order + [n // 2]


def body(
    NZ, NX,
    ends, hidden, queries, gain, w_own, w_give, bias, cos_t, sin_t,
    out,
    wbuf, hbuf, nbuf, acc, kvown, qbuf, buf, obuf,
    pair_s, pair_r, own_s, zs, zr, xs, xr, hs, hr, gs, gr, qs, qr,
    ks, kr, ds, dr, fs, fr, os, orr,
):
    NP = NZ // 2
    ZH, XH = NP // 2, NX // 2
    z = lax.axis_index("sp")
    x = lax.axis_index("blk")
    r = lax.axis_index("rep")
    p = z // 2
    b = lax.rem(z, 2)
    rows = hidden.shape[0]
    half = rows // 2

    def mod(a, n):
        return lax.rem(a + 2 * n, n)

    def at(sp=None, blk=None, rep=None):
        return {
            "sp": z if sp is None else sp,
            "blk": x if blk is None else blk,
            "rep": r if rep is None else rep,
        }

    def remote(src, dst, ss, rs, dev):
        return pltpu.make_async_remote_copy(
            src_ref=src, dst_ref=dst, send_sem=ss, recv_sem=rs,
            device_id=dev, device_id_type=MESH,
        )

    barrier = pltpu.get_barrier_semaphore()
    for j in range(1, 2 * NZ):
        other = mod(2 * z + r + j, 2 * NZ)
        pl.semaphore_signal(
            barrier, inc=1, device_id=at(sp=other // 2, rep=lax.rem(other, 2)),
            device_id_type=MESH,
        )
    for dx in (1, -1):
        pl.semaphore_signal(
            barrier, inc=1, device_id=at(blk=mod(x + dx, NX)), device_id_type=MESH
        )
    pl.semaphore_wait(barrier, 2 * NZ + 1)

    slice_rows = wbuf.shape[3]
    mine = pl.ds(pl.multiple_of(x * slice_rows, slice_rows), slice_rows)
    partner = z + 1 - 2 * b

    give = remote(w_give.at[mine], wbuf.at[p, b, x], pair_s, pair_r, at(sp=partner))
    give.start()
    own = pltpu.make_async_copy(w_own.at[mine], wbuf.at[p, b, x], own_s)
    own.start()

    def z_send(h, d):
        item = mod(p - (h - 1) if d == 0 else p + (h - 1), NP)
        ref = wbuf.at[item, :, x] if h < ZH else wbuf.at[item, d, x]
        to = mod(z + 2 if d == 0 else z - 2, NZ)
        return remote(ref, ref, zs.at[d, h - 1], zr.at[d, h - 1], at(sp=to))

    def z_recv(h, d):
        item = mod(p - h if d == 0 else p + h, NP)
        ref = wbuf.at[item, :, x] if h < ZH else wbuf.at[item, d, x]
        return remote(ref, ref, zs.at[d, h - 1], zr.at[d, h - 1], at(sp=mod(z + 2, NZ)))

    offs = ring_offsets(NP)

    def x_send(i, h, d):
        item = mod(p + offs[i], NP)
        sl = mod(x - (h - 1) if d == 0 else x + (h - 1), NX)
        ref = wbuf.at[item, :, sl] if h < XH else wbuf.at[item, d, sl]
        to = mod(x + 1 if d == 0 else x - 1, NX)
        return remote(ref, ref, xs.at[i, d, h - 1], xr.at[i, d, h - 1], at(blk=to))

    def x_recv(i, h, d):
        item = mod(p + offs[i], NP)
        sl = mod(x - h if d == 0 else x + h, NX)
        ref = wbuf.at[item, :, sl] if h < XH else wbuf.at[item, d, sl]
        return remote(ref, ref, xs.at[i, d, h - 1], xr.at[i, d, h - 1], at(blk=mod(x + 1, NX)))

    HC = hs.shape[0]
    hrows = half // HC

    def h_send(k):
        ref_rows = pl.ds(pl.multiple_of(r * half + k * hrows, hrows), hrows)
        return remote(hidden.at[ref_rows], hbuf.at[ref_rows], hs.at[k], hr.at[k], at(sp=partner))

    def h_relay(k):
        ref_rows = pl.ds(pl.multiple_of(r * half + k * hrows, hrows), hrows)
        return remote(hbuf.at[ref_rows], hbuf.at[ref_rows], gs.at[k], gr.at[k], at(rep=1 - r))

    def h_relayed(k):
        ref_rows = pl.ds(pl.multiple_of((1 - r) * half + k * hrows, hrows), hrows)
        return remote(hbuf.at[ref_rows], hbuf.at[ref_rows], gs.at[k], gr.at[k], at(rep=1 - r))

    QN = queries.shape[1] // HEAD

    def start_q(j):
        hl = mod(2 * lax.rem(p, QN // 2) + j, QN)
        dz = r * (QN // 2) + hl // 2
        dc = lax.rem(hl, 2)
        src = queries.at[:, pl.ds(pl.multiple_of(hl * HEAD, HEAD), HEAD)]
        dst = qbuf.at[pl.ds(pl.multiple_of(z * rows, rows), rows)]
        self_case = (dz == z) & (dc == r)

        @pl.when(self_case)
        def _():
            pltpu.make_async_copy(src, dst, qr.at[z]).start()

        @pl.when(jnp.logical_not(self_case))
        def _():
            remote(src, dst, qs.at[j], qr.at[z], at(sp=dz, rep=dc)).start()

    def finish_q_send(j):
        hl = mod(2 * lax.rem(p, QN // 2) + j, QN)
        dz = r * (QN // 2) + hl // 2
        dc = lax.rem(hl, 2)
        src = queries.at[:, pl.ds(pl.multiple_of(hl * HEAD, HEAD), HEAD)]
        dst = qbuf.at[pl.ds(pl.multiple_of(z * rows, rows), rows)]

        @pl.when(jnp.logical_not((dz == z) & (dc == r)))
        def _():
            remote(src, dst, qs.at[j], qr.at[z], at(sp=dz, rep=dc)).wait_send()

    def norm_into(src, row0):
        step = 16

        def one(k, _):
            at_rows = pl.ds(pl.multiple_of(k * step, step), step)
            v = src[at_rows, :].astype(F32)
            scale = lax.rsqrt(jnp.mean(v * v, axis=1, keepdims=True) + EPS_VALUE)
            nbuf[pl.ds(pl.multiple_of(row0 + k * step, step), step), :] = (
                v * scale * gain[...]
            ).astype(BF16)
            return 0

        lax.fori_loop(0, rows // step, one, 0)

    WK = wbuf.shape[1] * wbuf.shape[2] * wbuf.shape[3]

    def dot_item(i, first):
        item = mod(p + offs[i], NP)
        lhs = nbuf[:, pl.ds(pl.multiple_of(item * WK, WK), WK)]
        w = wbuf[item].reshape(WK, wbuf.shape[4])
        d = jnp.dot(lhs, w, preferred_element_type=F32)
        if first:
            acc[...] = d
        else:
            acc[...] += d

    own.wait()
    give.wait_recv()
    last = NP + XH - 1
    done_dots = 0
    q_next = 0
    for t in range(last + 1):
        if t < ZH:
            for d in (0, 1):
                if t:
                    z_recv(t, d).wait_recv()
                z_send(t + 1, d).start()
        elif t == ZH:
            for d in (0, 1):
                z_recv(ZH, d).wait_recv()
        for h in range(1, XH + 1):
            i = t - (h - 1)
            if 0 <= i < NP:
                for d in (0, 1):
                    if h > 1:
                        x_recv(i, h - 1, d).wait_recv()
                    x_send(i, h, d).start()
        if t < HC:
            h_send(t).start()
        if t == 0:
            norm_into(hidden, b * rows)
        if 1 <= t <= HC:
            h_send(t - 1).wait_recv()
            h_relay(t - 1).start()
        if t >= 1:
            for _ in range(3):
                if q_next < QN:
                    start_q(q_next)
                    q_next += 1
        if t == HC + 2:
            for k in range(HC):
                h_relayed(k).wait_recv()
            norm_into(hbuf, (1 - b) * rows)
        if t >= HC + 3:
            while done_dots + XH <= t:
                for d in (0, 1):
                    x_recv(done_dots, XH, d).wait_recv()
                dot_item(done_dots, done_dots == 0)
                done_dots += 1
    while q_next < QN:
        start_q(q_next)
        q_next += 1
    while done_dots < NP:
        for d in (0, 1):
            x_recv(done_dots, XH, d).wait_recv()
        dot_item(done_dots, done_dots == 0)
        done_dots += 1

    NH = kvown.shape[0]
    for j in range(NH):
        cols = slice(j * HEAD, (j + 1) * HEAD)
        y = acc[:, cols] + bias[:, cols]
        kvown[j] = (y * cos_t[...] + pltpu.roll(y, HEAD // 2, 1) * sin_t[...]).astype(BF16)

    g = z // 2

    def start_kv(k):
        k2 = mod(k + 2 * lax.rem(p, NH), 2 * NH)
        j, e = k2 // 2, lax.rem(k2, 2)
        dz = 2 * (NH * r + j) + e
        src = kvown.at[j]
        dst = buf.at[b, 2 * NP + p]
        self_case = (dz == z) & (b == r)

        @pl.when(self_case)
        def _():
            pltpu.make_async_copy(src, dst, kr.at[p]).start()

        @pl.when(jnp.logical_not(self_case))
        def _():
            remote(src, dst, ks.at[k], kr.at[p], at(sp=dz, rep=b)).start()

    def finish_kv_send(k):
        k2 = mod(k + 2 * lax.rem(p, NH), 2 * NH)
        j, e = k2 // 2, lax.rem(k2, 2)
        dz = 2 * (NH * r + j) + e

        @pl.when(jnp.logical_not((dz == z) & (b == r)))
        def _():
            remote(kvown.at[j], buf.at[b, 2 * NP + p], ks.at[k], kr.at[p], at(sp=dz, rep=b)).wait_send()

    for k in range(2 * NH):
        start_kv(k)

    def relay(a, i):
        q = mod(g + offs[i], NP)
        here = buf.at[r, (2 - a) * NP + q]
        if a == 0:
            remote(here, here, ks.at[0], kr.at[q], at()).wait_recv()
        else:
            remote(here, here, fs.at[a - 1, i], fr.at[a - 1, i], at()).wait_recv()
        remote(here, here, ds.at[a, i], dr.at[a, i], at(rep=1 - r)).start()
        if a < 2:
            there = buf.at[r, (1 - a) * NP + q]
            remote(here, there, fs.at[a, i], fr.at[a, i], at(blk=mod(x + 1, NX))).start()

    def relayed(a, i):
        q = mod(g + offs[i], NP)
        ref = buf.at[1 - r, (2 - a) * NP + q]
        remote(ref, ref, ds.at[a, i], dr.at[a, i], at(rep=1 - r)).wait_recv()

    for i in range(NP):
        relay(0, i)
    for a in (1, 2):
        for i in range(NP):
            relay(a, i)
    for a in (0, 1, 2):
        for i in range(NP):
            relayed(a, i)
    for zz in range(NZ):
        ref = qbuf.at[pl.ds(zz * rows, rows)]
        remote(ref, ref, qs.at[0], qr.at[zz], at()).wait_recv()

    NT = qbuf.shape[0] // TILE
    per = TILE // rows
    span = qbuf.shape[0]
    units = TILE // buf.shape[2]
    factor = math.log2(math.e) / math.sqrt(HEAD)
    ones = jnp.ones((TILE, HEAD), BF16)
    col = lax.broadcasted_iota(jnp.int32, (TILE, TILE), 1)
    row = lax.broadcasted_iota(jnp.int32, (TILE, TILE), 0)
    oc = z // (NZ // 2)
    olane = lax.rem(2 * z + r, QN)

    def out_copy(qi, k):
        dz = qi * per + k
        src = obuf.at[qi, pl.ds(k * rows, rows)]
        dst = out.at[:, pl.ds(pl.multiple_of(olane * HEAD, HEAD), HEAD)]
        return dz, src, dst, (dz == z) & (oc == r)

    def q_tile(n, _):
        shift = jnp.where(n == 0, 2, jnp.where(n == 1, 1, jnp.where(n == 2, 3, 0)))
        qi = lax.rem(z // per + shift, NT)
        q = qbuf[pl.ds(pl.multiple_of(qi * TILE, TILE), TILE), :]
        pos = x * span + qi * TILE + lax.broadcasted_iota(jnp.int32, (TILE, HEAD), 0)
        lo = jnp.zeros((TILE, HEAD), jnp.int32)
        for d in range(ends.shape[0]):
            lo = jnp.where(pos >= ends[d], ends[d], lo)
        m = None
        for back in range(2 * NT + 1):
            tile = 2 * NT + qi - back
            kk = buf[0, pl.ds(tile * units, units)].reshape(TILE, HEAD)
            vv = buf[1, pl.ds(tile * units, units)].reshape(TILE, HEAD)
            s = lax.dot_general(q, kk, (((1,), (1,)), ((), ())), preferred_element_type=F32)
            base = x * span + (qi - back) * TILE
            low = jnp.concatenate([lo - base] * (TILE // HEAD), axis=1)
            seen = col >= low
            if back == 0:
                seen = seen & (col <= row)
            s = jnp.where(seen, s, NEG_FILL)
            top = jnp.broadcast_to(jnp.max(s, axis=1, keepdims=True), (TILE, HEAD))
            m_new = top if m is None else jnp.maximum(m, top)
            w = jnp.exp2(
                (s - jnp.concatenate([m_new] * (TILE // HEAD), axis=1)) * factor
            ).astype(BF16)
            pv = jnp.dot(w, jnp.concatenate([vv, ones], axis=1), preferred_element_type=F32)
            if m is None:
                total = pv
            else:
                alpha = jnp.exp2((m - m_new) * factor)
                total = total * jnp.concatenate([alpha, alpha], axis=1) + pv
            m = m_new
        obuf[qi] = (total[:, :HEAD] / total[:, HEAD:]).astype(BF16)
        for k in range(per):
            dz, src, dst, self_case = out_copy(qi, k)

            @pl.when(self_case)
            def _():
                pltpu.make_async_copy(src, dst, orr.at[olane]).start()

            @pl.when(jnp.logical_not(self_case))
            def _():
                remote(src, dst, os.at[qi, k], orr.at[olane], at(sp=dz, rep=oc)).start()

        return 0

    lax.fori_loop(0, NT, q_tile, 0)

    for hl in range(QN):
        ref = out.at[:, pl.ds(hl * HEAD, HEAD)]
        remote(ref, ref, os.at[0, 0], orr.at[hl], at()).wait_recv()
    for qi in range(NT):
        for k in range(per):
            dz, src, dst, self_case = out_copy(qi, k)

            @pl.when(jnp.logical_not(self_case))
            def _():
                remote(src, dst, os.at[qi, k], orr.at[olane], at(sp=dz, rep=oc)).wait_send()

    give.wait_send()
    for h in range(1, ZH + 1):
        for d in (0, 1):
            z_send(h, d).wait_send()
    for i in range(NP):
        for h in range(1, XH + 1):
            for d in (0, 1):
                x_send(i, h, d).wait_send()
    for k in range(HC):
        h_send(k).wait_send()
        h_relay(k).wait_send()
    for j in range(QN):
        finish_q_send(j)
    for k in range(2 * NH):
        finish_kv_send(k)
    for a in (0, 1, 2):
        for i in range(NP):
            q = mod(g + offs[i], NP)
            here = buf.at[r, (2 - a) * NP + q]
            remote(here, here, ds.at[a, i], dr.at[a, i], at(rep=1 - r)).wait_send()
            if a < 2:
                remote(here, here, fs.at[a, i], fr.at[a, i], at()).wait_send()


def on_device(
    hidden, queries, norm_gain, key_matrix, value_matrix, key_shift_bias, value_shift_bias,
    doc_lengths,
):
    NZ, NX = lax.axis_size("sp"), lax.axis_size("blk")
    NP = NZ // 2
    z, x = lax.axis_index("sp"), lax.axis_index("blk")
    rows, width = hidden.shape[1:]
    span = rows * NZ
    krows, kcols = key_matrix.shape
    heads = kcols // HEAD
    even = lax.rem(z, 2) == 0
    w_own = jnp.where(even, key_matrix, value_matrix)
    w_give = jnp.where(even, value_matrix, key_matrix)
    bias = jnp.where(even, key_shift_bias, value_shift_bias).astype(F32)[None]
    places = (x * span + (z // 2) * 2 * rows + jnp.arange(2 * rows)).astype(F32)
    freq = jnp.arange(HEAD // 2).astype(F32)
    inverse = jnp.exp(freq * (-2.0 * math.log(THETA_BASE) / HEAD))
    angles = places[:, None] * inverse[None, :]
    cosine, sine = jnp.cos(angles), jnp.sin(angles)
    cos_t = jnp.where(even, jnp.concatenate([cosine, cosine], 1), 1.0)
    sin_t = jnp.where(even, jnp.concatenate([-sine, sine], 1), 0.0)
    ends = jnp.cumsum(doc_lengths).astype(jnp.int32)
    HC = 4
    QN = queries.shape[2] // HEAD
    NT = span // TILE
    dma = pltpu.SemaphoreType.DMA
    vmem = pl.BlockSpec(memory_space=pltpu.VMEM)
    out = pl.pallas_call(
        functools.partial(body, NZ, NX),
        out_shape=jax.ShapeDtypeStruct((rows, queries.shape[2]), BF16),
        in_specs=[pl.BlockSpec(memory_space=pltpu.SMEM)] + [vmem] * 8,
        out_specs=vmem,
        scratch_shapes=[
            pltpu.VMEM((NP, 2, NX, krows // NX, kcols), BF16),
            pltpu.VMEM((rows, width), BF16),
            pltpu.VMEM((2 * rows, width), BF16),
            pltpu.VMEM((2 * rows, kcols), F32),
            pltpu.VMEM((heads, 2 * rows, HEAD), BF16),
            pltpu.VMEM((span, HEAD), BF16),
            pltpu.VMEM((2, 3 * NP, 2 * rows, HEAD), BF16),
            pltpu.VMEM((NT, TILE, HEAD), BF16),
            dma(()), dma(()), dma(()),
            dma((2, NP // 2)), dma((2, NP // 2)),
            dma((NP, 2, NX // 2)), dma((NP, 2, NX // 2)),
            dma((HC,)), dma((HC,)), dma((HC,)), dma((HC,)),
            dma((QN,)), dma((NZ,)),
            dma((2 * heads,)), dma((NP,)),
            dma((3, NP)), dma((3, NP)),
            dma((2, NP)), dma((2, NP)),
            dma((NT, TILE // rows)), dma((QN,)),
        ],
        compiler_params=pltpu.CompilerParams(
            collective_id=0, has_side_effects=True, vmem_limit_bytes=56 * 2**20
        ),
    )(
        ends, hidden[0], queries[0], norm_gain[None].astype(F32), w_own, w_give, bias,
        cos_t, sin_t,
    )
    return out[None]


def solution(mesh):
    in_specs = (
        P(("grp", "blk"), "sp", None),
        P(("grp", "blk"), "sp", "rep"),
        P(),
        P("sp", "rep"),
        P("sp", "rep"),
        P("rep"),
        P("rep"),
        P("grp"),
    )
    out_specs = P(("grp", "blk"), "sp", "rep")
    return jax.shard_map(
        on_device, mesh=mesh, in_specs=in_specs, out_specs=out_specs, check_vma=False
    )
```

time: 468 us -> 197 us (0.42)
  the two profiles are of different devices: /device:TPU:88 before, /device:TPU:80 now
where the time goes in v1:
time: 197 us
  Pallas kernels  190 us (96%)
  other arithmetic  3.48 us (2%)
  local copies, waits for them, and re-layouts  3.39 us (2%)
    pallas_call x1, Pallas kernels, on_device(): pl.pallas_call(functools.partial(body, NZ, NX), out_shape=jax.ShapeDtypeS...  190 us

profile of v1, /device:TPU:80, one launch (start us, length us, event | category | flops | bytes accessed | tf_op | source)
XLA Modules:
  0.0 196.6 jit_solution(2305509544761896074)
XLA Ops:
  0.0 0.0 copy-start.4
  0.0 0.7 copy-done.4
  0.7 0.7 reduce-window.9
  1.4 0.0 copy-start.3
  1.4 0.0 copy-start.2
  1.4 0.7 copy-done.3
  2.0 0.0 copy-done.2
  2.1 0.6 select_convert_fusion
  2.6 0.5 fusion
  3.2 0.0 copy-start
  3.2 0.0 copy-start.1
  3.2 0.8 maximum_select_fusion
  4.0 0.1 copy-done
  4.1 0.1 copy-done.1
  4.2 0.8 broadcast_select_fusion
  5.0 189.7 %shard_map.82 = bf16[128,2048]{1,0:T(8,128)(2,1)} custom-call(s32[8]{0:T(128)} %bitcast.12, bf16[128,4096]{1,0:T(8,128)(2,1)} %bitcast.8, bf16[128,2048]{1,0:T(8,128)(2,1)} %bitcast.9, f32[1,4096]{1,0:T(1,128)} %bitcast.10, bf16[256,512]{1,0:T(8,128)(2,1)} %get-tuple-element.6.w_own, bf16[256,512]{1,0:T(8,128)(2,1)} %get-tuple-element.5.w_give, ...), custom_call_target="tpu_custom_call" | custom-call | tf_op jit(solution)/shard_map/pallas_call | solution.py:425
  194.8 1.9 copy.10
  (2 shorter events, 0.0 us)
Async XLA Ops:
  0.0 0.7 copy-start.4
  1.4 0.7 copy-start.3
  1.4 0.7 copy-start.2
  3.2 1.0 copy-start
  3.2 1.0 copy-start.1

commit v2 on v1

v2 whole, which is shorter than its diff:
```python
import functools
import math

import jax
import jax.numpy as jnp
from jax import lax
from jax.experimental import pallas as pl
from jax.experimental.pallas import tpu as pltpu
from jax.sharding import PartitionSpec as P

HEAD = 128
EPS_VALUE = 1e-06
THETA_BASE = 1000000.0
NEG_FILL = -1e30
KEY_TILE = 512
MESH = pl.DeviceIdType.MESH
F32 = jnp.float32
BF16 = jnp.bfloat16


def ring_offsets(n):
    order = [0]
    for k in range(1, n // 2):
        order += [-k, k]
    return order + [n // 2]


def body(
    NZ, NX,
    lengths, hidden, queries, gain, wk, wv, bias, cos_t, sin_t,
    out,
    wbuf, hown, hbuf, nbuf, acc, kvown, qbuf, buf, obuf,
    pair_s, pair_r, own_s, hown_s, zs, zr, xs, xr, hs, hr, gs, gr, qs, qr,
    ks, kr, ds, dr, fs, fr, os, orr,
):
    NP = NZ // 2
    ZH, XH = NP // 2, NX // 2
    z = lax.axis_index("sp")
    x = lax.axis_index("blk")
    r = lax.axis_index("rep")
    p = z // 2
    b = lax.rem(z, 2)
    rows = hidden.shape[0]
    half = rows // 2

    def mod(a, n):
        return lax.rem(a + 2 * n, n)

    def at(sp=None, blk=None, rep=None):
        return {
            "sp": z if sp is None else sp,
            "blk": x if blk is None else blk,
            "rep": r if rep is None else rep,
        }

    def remote(src, dst, ss, rs, dev):
        return pltpu.make_async_remote_copy(
            src_ref=src, dst_ref=dst, send_sem=ss, recv_sem=rs,
            device_id=dev, device_id_type=MESH,
        )

    def drain(ref, sem):
        pltpu.make_async_copy(ref, ref, sem).wait()

    def signal(sem, dev):
        pl.semaphore_signal(sem, inc=1, device_id=dev, device_id_type=MESH)

    barrier = pltpu.get_barrier_semaphore()
    for j in range(1, 2 * NZ):
        other = mod(2 * z + r + j, 2 * NZ)
        signal(barrier, at(sp=other // 2, rep=lax.rem(other, 2)))
    for dx in (1, -1):
        signal(barrier, at(blk=mod(x + dx, NX)))

    slice_rows = wbuf.shape[3]
    mine = pl.ds(pl.multiple_of(x * slice_rows, slice_rows), slice_rows)
    partner = z + 1 - 2 * b
    own_slot = wbuf.at[p, b, x]

    @pl.when(b == 0)
    def _():
        pltpu.make_async_copy(wk.at[mine], own_slot, own_s).start()

    @pl.when(b == 1)
    def _():
        pltpu.make_async_copy(wv.at[mine], own_slot, own_s).start()

    pltpu.make_async_copy(hidden, hown, hown_s).start()
    pl.semaphore_wait(barrier, 2 * NZ + 1)

    @pl.when(b == 0)
    def _():
        remote(wv.at[mine], own_slot, pair_s, pair_r, at(sp=partner)).start()

    @pl.when(b == 1)
    def _():
        remote(wk.at[mine], own_slot, pair_s, pair_r, at(sp=partner)).start()

    give = remote(wk.at[mine], own_slot, pair_s, pair_r, at(sp=partner))

    items = [mod(p + o, NP) for o in ring_offsets(NP)]

    def z_send(h, d):
        item = mod(p - (h - 1) if d == 0 else p + (h - 1), NP)
        ref = wbuf.at[item, :, x] if h < ZH else wbuf.at[item, d, x]
        to = mod(z + 2 if d == 0 else z - 2, NZ)
        return remote(ref, ref, zs, zr.at[d, h - 1], at(sp=to))

    def z_recv(h, d):
        item = mod(p - h if d == 0 else p + h, NP)
        ref = wbuf.at[item, :, x] if h < ZH else wbuf.at[item, d, x]
        return remote(ref, ref, zs, zr.at[d, h - 1], at(sp=mod(z + 2, NZ)))

    def x_send(i, h, d):
        sl = mod(x - (h - 1) if d == 0 else x + (h - 1), NX)
        ref = wbuf.at[items[i], :, sl] if h < XH else wbuf.at[items[i], d, sl]
        to = mod(x + 1 if d == 0 else x - 1, NX)
        return remote(ref, ref, xs, xr.at[i, d, h - 1], at(blk=to))

    def x_recv(i, h, d):
        sl = mod(x - h if d == 0 else x + h, NX)
        ref = wbuf.at[items[i], :, sl] if h < XH else wbuf.at[items[i], d, sl]
        return remote(ref, ref, xs, xr.at[i, d, h - 1], at(blk=mod(x + 1, NX)))

    HC = hr.shape[0]
    hrows = half // HC

    def h_send(k):
        ref_rows = pl.ds(pl.multiple_of(r * half + k * hrows, hrows), hrows)
        return remote(hidden.at[ref_rows], hbuf.at[ref_rows], hs, hr.at[k], at(sp=partner))

    def h_relay(k):
        ref_rows = pl.ds(pl.multiple_of(r * half + k * hrows, hrows), hrows)
        return remote(hbuf.at[ref_rows], hbuf.at[ref_rows], gs, gr, at(rep=1 - r))

    QN = queries.shape[1] // HEAD

    def q_case(j):
        hl = mod(2 * lax.rem(p, QN // 2) + j, QN)
        dz = r * (QN // 2) + hl // 2
        dc = lax.rem(hl, 2)
        src = queries.at[:, pl.ds(pl.multiple_of(hl * HEAD, HEAD), HEAD)]
        dst = qbuf.at[pl.ds(pl.multiple_of(z * rows, rows), rows)]
        return src, dst, at(sp=dz, rep=dc), (dz == z) & (dc == r)

    def start_q(j):
        src, dst, dev, self_case = q_case(j)

        @pl.when(self_case)
        def _():
            pltpu.make_async_copy(src, dst, qr).start()

        @pl.when(jnp.logical_not(self_case))
        def _():
            remote(src, dst, qs, qr, dev).start()

    def norm_into(src, row0):
        step = 16

        def one(k, _):
            at_rows = pl.ds(pl.multiple_of(k * step, step), step)
            v = src[at_rows, :].astype(F32)
            scale = lax.rsqrt(jnp.mean(v * v, axis=1, keepdims=True) + EPS_VALUE)
            nbuf[pl.ds(pl.multiple_of(row0 + k * step, step), step), :] = (
                v * scale * gain[...]
            ).astype(BF16)
            return 0

        lax.fori_loop(0, rows // step, one, 0)

    WK = wbuf.shape[1] * wbuf.shape[2] * wbuf.shape[3]

    def dot_item(i, first):
        lhs = nbuf[:, pl.ds(pl.multiple_of(items[i] * WK, WK), WK)]
        w = wbuf[items[i]].reshape(WK, wbuf.shape[4])
        d = jnp.dot(lhs, w, preferred_element_type=F32)
        if first:
            acc[...] = d
        else:
            acc[...] += d

    pltpu.make_async_copy(wk.at[mine], own_slot, own_s).wait()
    give.wait_recv()
    last = NP + XH - 1
    done_dots = 0
    q_next = 0
    q_ticks = [0] * (last + 1)
    for n in range(QN):
        q_ticks[min(ZH + n // 3, last)] += 1
    for t in range(last + 1):
        with jax.named_scope(f"t{t}"):
            for h in range(XH, 0, -1):
                if h == 1:
                    if 1 <= t <= ZH:
                        for d in (0, 1):
                            z_recv(t, d).wait_recv()
                    if t < ZH:
                        for d in (0, 1):
                            z_send(t + 1, d).start()
                i = t - (h - 1)
                if 0 <= i < NP:
                    for d in (0, 1):
                        if h > 1:
                            x_recv(i, h - 1, d).wait_recv()
                        x_send(i, h, d).start()
            if t < HC:
                h_send(t).start()
            if t == 0:
                pltpu.make_async_copy(hidden, hown, hown_s).wait()
                norm_into(hown, b * rows)
            for _ in range(q_ticks[t]):
                start_q(q_next)
                q_next += 1
            if 3 <= t < HC + 3:
                h_send(t - 3).wait_recv()
                h_relay(t - 3).start()
            if t == HC + 4:
                drain(hbuf.at[pl.ds(pl.multiple_of((1 - r) * half, half), half)], gr)
                norm_into(hbuf, (1 - b) * rows)
            if t >= HC + 4:
                for _ in range(2 if t < last else NP):
                    if done_dots < NP and done_dots + XH <= t:
                        for d in (0, 1):
                            x_recv(done_dots, XH, d).wait_recv()
                        dot_item(done_dots, done_dots == 0)
                        done_dots += 1
    assert done_dots == NP and q_next == QN

    NH = kvown.shape[0]
    for j in range(NH):
        cols = slice(j * HEAD, (j + 1) * HEAD)

        @pl.when(b == 0)
        def _():
            y = acc[:, cols] + bias[0:1, cols]
            kvown[j] = (y * cos_t[...] + pltpu.roll(y, HEAD // 2, 1) * sin_t[...]).astype(BF16)

        @pl.when(b == 1)
        def _():
            kvown[j] = (acc[:, cols] + bias[1:2, cols]).astype(BF16)

    prow = 2 * rows
    span = rows * NZ

    def unit(a, q):
        return pl.ds(pl.multiple_of((2 - a) * span + q * prow, prow), prow)

    def kv_case(k):
        j, e = lax.rem(k // 2 + p, NH), k % 2
        dz = 2 * (NH * r + j) + e
        return kvown.at[j], buf.at[b, unit(0, p)], at(sp=dz, rep=b), (dz == z) & (b == r)

    def start_kv(k):
        src, dst, dev, self_case = kv_case(k)

        @pl.when(self_case)
        def _():
            pltpu.make_async_copy(src, dst, kr.at[p]).start()

        @pl.when(jnp.logical_not(self_case))
        def _():
            remote(src, dst, ks, kr.at[p], dev).start()

    for k in range(2 * NH):
        start_kv(k)

    def relay(a, q):
        here = buf.at[r, unit(a, q)]
        if a == 0:
            remote(here, here, ks, kr.at[q], at()).wait_recv()
        else:
            remote(here, here, fs, fr.at[a - 1, q], at()).wait_recv()
        remote(here, here, ds, dr, at(rep=1 - r)).start()
        if a < 2:
            there = buf.at[r, unit(a + 1, q)]
            remote(here, there, fs, fr.at[a, q], at(blk=mod(x + 1, NX))).start()

    pairs = []
    for k in range(NH):
        first = mod(p - k, NH)
        pairs += [first + NH * c for c in range(NP // NH)]
    for i in range(NP + 2):
        with jax.named_scope(f"relay{i}"):
            for a in (0, 1, 2):
                if 0 <= i - a < NP:
                    relay(a, pairs[i - a])
    with jax.named_scope("relayed"):
        drain(buf.at[1 - r], dr)
        drain(qbuf, qr)

    KT = KEY_TILE // rows
    factor = math.log2(math.e) / math.sqrt(HEAD)
    ones = jnp.ones((KEY_TILE, HEAD), BF16)
    oc = z // (NZ // 2)
    olane = lax.rem(2 * z + r, QN)
    odst = out.at[:, pl.ds(pl.multiple_of(olane * HEAD, HEAD), HEAD)]

    def q_tile(qi):
        q = qbuf[pl.ds(pl.multiple_of(qi * rows, rows), rows), :]
        first = x * span + qi * rows
        pos = first + lax.broadcasted_iota(jnp.int32, (rows, HEAD), 0)
        lo = jnp.zeros((rows, HEAD), jnp.int32)
        end = jnp.int32(0)
        for d in range(lengths.shape[0]):
            end = end + lengths[d]
            lo = jnp.where(pos >= end, end, lo)
        lo = lo - first
        m = None
        for back in range(2 * NZ // KT + 1):
            n = rows if back == 0 else KEY_TILE
            at_rows = pl.ds(pl.multiple_of(2 * span + qi * rows - back * KEY_TILE, rows), n)
            s = lax.dot_general(
                q, buf[0, at_rows, :], (((1,), (1,)), ((), ())), preferred_element_type=F32
            )
            col = lax.broadcasted_iota(jnp.int32, (rows, n), 1)
            low = lo + back * KEY_TILE
            seen = col >= jnp.concatenate([low] * (n // HEAD), axis=1)
            if back == 0:
                seen = seen & (col <= lax.broadcasted_iota(jnp.int32, (rows, n), 0))
            s = jnp.where(seen, s, NEG_FILL)
            top = jnp.broadcast_to(jnp.max(s, axis=1, keepdims=True), (rows, HEAD))
            m_new = top if m is None else jnp.maximum(m, top)
            w = jnp.exp2((s - jnp.concatenate([m_new] * (n // HEAD), axis=1)) * factor).astype(BF16)
            vv = jnp.concatenate([buf[1, at_rows, :], ones[:n]], axis=1)
            pv = jnp.dot(w, vv, preferred_element_type=F32)
            if m is None:
                total = pv
            else:
                alpha = jnp.exp2((m - m_new) * factor)
                total = total * jnp.concatenate([alpha, alpha], axis=1) + pv
            m = m_new
        obuf[pl.ds(pl.multiple_of(qi * rows, rows), rows), :] = (
            total[:, :HEAD] / total[:, HEAD:]
        ).astype(BF16)

    def send_out(dz):
        src = obuf.at[pl.ds(pl.multiple_of(dz * rows, rows), rows)]
        self_case = (dz == z) & (oc == r)

        @pl.when(self_case)
        def _():
            pltpu.make_async_copy(src, odst, orr).start()

        @pl.when(jnp.logical_not(self_case))
        def _():
            remote(src, odst, os, orr, at(sp=dz, rep=oc)).start()

    def q_pair(n, _):
        with jax.named_scope("qtile"):
            for qi in (n, n + NZ // 2):
                q_tile(qi)
            for qi in (n, n + NZ // 2):
                send_out(qi)
        return 0

    lax.fori_loop(0, NZ // 2, q_pair, 0)

    with jax.named_scope("owait"):
        drain(out, orr)
    with jax.named_scope("sends"):
        give.wait_send()
        drain(wbuf.at[pl.ds(0, NP - 1), :, 0], zs)
        drain(wbuf.at[:, :, pl.ds(0, NX - 1)], xs)
        drain(hidden.at[pl.ds(0, half)], hs)
        drain(hidden.at[pl.ds(0, half)], gs)
        drain(buf.at[0], ds)
        drain(buf.at[0, pl.ds(0, 2 * span)], fs)

        q_self = r == z // (NZ // 2)
        for sem in (qs, os):

            @pl.when(q_self)
            def _():
                drain(qbuf.at[pl.ds(0, span - rows)], sem)

            @pl.when(jnp.logical_not(q_self))
            def _():
                drain(qbuf, sem)

        kv_self = q_self & (b == r)

        @pl.when(kv_self)
        def _():
            drain(buf.at[0, pl.ds(0, (2 * NH - 1) * prow)], ks)

        @pl.when(jnp.logical_not(kv_self))
        def _():
            drain(buf.at[0, pl.ds(0, 2 * NH * prow)], ks)


def on_device(
    hidden, queries, norm_gain, key_matrix, value_matrix, key_shift_bias, value_shift_bias,
    doc_lengths,
):
    NZ, NX = lax.axis_size("sp"), lax.axis_size("blk")
    NP = NZ // 2
    z, x = lax.axis_index("sp"), lax.axis_index("blk")
    rows, width = hidden.shape[1:]
    span = rows * NZ
    krows, kcols = key_matrix.shape
    heads = kcols // HEAD
    places = (x * span + (z // 2) * 2 * rows + jnp.arange(2 * rows)).astype(F32)
    lane = jnp.arange(HEAD)
    freq = (lane % (HEAD // 2)).astype(F32)
    inverse = jnp.exp(freq * (-2.0 * math.log(THETA_BASE) / HEAD))
    angles = places[:, None] * inverse[None, :]
    cos_t = jnp.cos(angles)
    sin_t = jnp.sin(angles) * jnp.where(lane < HEAD // 2, -1.0, 1.0).astype(F32)
    bias = jnp.stack([key_shift_bias, value_shift_bias]).astype(F32)
    HC = 4
    QN = queries.shape[2] // HEAD
    dma = pltpu.SemaphoreType.DMA
    vmem = pl.BlockSpec(memory_space=pltpu.VMEM)
    hbm = pl.BlockSpec(memory_space=pl.ANY)
    out = pl.pallas_call(
        functools.partial(body, NZ, NX),
        out_shape=jax.ShapeDtypeStruct((rows, queries.shape[2]), BF16),
        in_specs=[pl.BlockSpec(memory_space=pltpu.SMEM), hbm, hbm, vmem, hbm, hbm] + [vmem] * 3,
        out_specs=hbm,
        scratch_shapes=[
            pltpu.VMEM((NP, 2, NX, krows // NX, kcols), BF16),
            pltpu.VMEM((rows, width), BF16),
            pltpu.VMEM((rows, width), BF16),
            pltpu.VMEM((2 * rows, width), BF16),
            pltpu.VMEM((2 * rows, kcols), F32),
            pltpu.VMEM((heads, 2 * rows, HEAD), BF16),
            pltpu.VMEM((span, HEAD), BF16),
            pltpu.VMEM((2, 3 * span, HEAD), BF16),
            pltpu.VMEM((span, HEAD), BF16),
            dma(()), dma(()), dma(()), dma(()),
            dma(()), dma((2, NP // 2)),
            dma(()), dma((NP, 2, NX // 2)),
            dma(()), dma((HC,)), dma(()), dma(()),
            dma(()), dma(()),
            dma(()), dma((NP,)),
            dma(()), dma(()),
            dma(()), dma((2, NP)),
            dma(()), dma(()),
        ],
        compiler_params=pltpu.CompilerParams(
            collective_id=0, has_side_effects=True, vmem_limit_bytes=56 * 2**20
        ),
    )(
        doc_lengths, hidden[0], queries[0], norm_gain[None], key_matrix, value_matrix,
        bias, cos_t, sin_t,
    )
    return out[None]


def solution(mesh):
    in_specs = (
        P(("grp", "blk"), "sp", None),
        P(("grp", "blk"), "sp", "rep"),
        P(),
        P("sp", "rep"),
        P("sp", "rep"),
        P("rep"),
        P("rep"),
        P("grp"),
    )
    out_specs = P(("grp", "blk"), "sp", "rep")
    return jax.shard_map(
        on_device, mesh=mesh, in_specs=in_specs, out_specs=out_specs, check_vma=False
    )
```

time: 197 us -> 182 us (0.924)
  Pallas kernels: 190 us -> 175 us
    pallas_call x1, Pallas kernels: 190 us -> 175 us  [on_device(): pl.pallas_call(functools.partial(body, NZ, NX), out_shape=jax.ShapeDtypeS...]
where the time goes in v2:
time: 182 us; the launch traced here: 180 us
  Pallas kernels  175 us (96%)
  local copies, waits for them, and re-layouts  3.24 us (2%)
  other arithmetic  1.85 us (1%)
    pallas_call x1, Pallas kernels, on_device(): pl.pallas_call(functools.partial(body, NZ, NX), out_shape=jax.ShapeDtypeS...  175 us

profile of v2, /device:TPU:80, one launch (start us, length us, event | category | flops | bytes accessed | tf_op | source)
XLA Modules:
  0.0 180.4 jit_solution(14164097702767196268)
XLA Ops:
  0.0 0.0 copy-start
  0.0 0.7 copy-done
  0.7 0.0 copy-start.1
  0.7 0.7 copy-done.1
  1.4 0.6 maximum_convert_fusion.bias
  2.0 1.2 fusion
  3.2 175.3 %shard_map.82 = bf16[128,2048]{1,0:T(8,128)(2,1)} custom-call(s32[8]{0:T(128)} %lengths.1, bf16[128,4096]{1,0:T(8,128)(2,1)} %bitcast.5, bf16[128,2048]{1,0:T(8,128)(2,1)} %bitcast.6, f32[1,4096]{1,0:T(1,128)} %bitcast.7, bf16[256,512]{1,0:T(8,128)(2,1)} %wk.1, bf16[256,512]{1,0:T(8,128)(2,1)} %wv.1, f32[2,512]{1,0:T(2,128)} %maximum_convert_fusion.bias, ...), custom_call_target="tpu_custom_call" | custom-call | tf_op jit(solution)/shard_map/pallas_call | solution.py:415
  178.5 1.9 %copy.10 = bf16[1,128,2048]{2,1,0:T(8,128)(2,1)} copy(bf16[1,128,2048]{2,1,0:T(8,128)(2,1)} %bitcast.4) | data formatting | bytes 1048576
  (4 shorter events, 0.0 us)
Async XLA Ops:
  0.0 0.7 copy-start
  0.7 0.7 copy-start.1

commit v3 on v2

--- a/solution.py
+++ b/solution.py
@@ -25,13 +25,26 @@
     return order + [n // 2]
 
 
+def near_first(count, ring):
+    return [
+        sorted(range(count), key=lambda c: min((c - k) % ring, (k - c) % ring)) for k in range(ring)
+    ]
+
+
+def pick(table, row, column):
+    value = jnp.int32(table[0][column])
+    for k in range(1, len(table)):
+        value = jnp.where(row == k, table[k][column], value)
+    return value
+
+
 def body(
     NZ, NX,
-    lengths, hidden, queries, gain, wk, wv, bias, cos_t, sin_t,
+    lengths, hidden, queries, gain, wk, wv, kb, vb, cos_t, sin_t,
     out,
     wbuf, hown, hbuf, nbuf, acc, kvown, qbuf, buf, obuf,
-    pair_s, pair_r, own_s, hown_s, zs, zr, xs, xr, hs, hr, gs, gr, qs, qr,
-    ks, kr, ds, dr, fs, fr, os, orr,
+    pair_s, pair_r, rest_s, rest_r, own_s, hown_s, zs, zr, xs, xr, hs, hr, gs, gr, qs, qr,
+    ks, kr, ps, ds, dr, fs, fr, os, orr,
 ):
     NP = NZ // 2
     ZH, XH = NP // 2, NX // 2
@@ -72,31 +85,32 @@
     for dx in (1, -1):
         signal(barrier, at(blk=mod(x + dx, NX)))
 
-    slice_rows = wbuf.shape[3]
-    mine = pl.ds(pl.multiple_of(x * slice_rows, slice_rows), slice_rows)
     partner = z + 1 - 2 * b
-    own_slot = wbuf.at[p, b, x]
+    own_slot = wbuf.at[p, b]
 
     @pl.when(b == 0)
     def _():
-        pltpu.make_async_copy(wk.at[mine], own_slot, own_s).start()
+        pltpu.make_async_copy(wk, own_slot, own_s).start()
 
     @pl.when(b == 1)
     def _():
-        pltpu.make_async_copy(wv.at[mine], own_slot, own_s).start()
+        pltpu.make_async_copy(wv, own_slot, own_s).start()
 
     pltpu.make_async_copy(hidden, hown, hown_s).start()
     pl.semaphore_wait(barrier, 2 * NZ + 1)
 
-    @pl.when(b == 0)
-    def _():
-        remote(wv.at[mine], own_slot, pair_s, pair_r, at(sp=partner)).start()
-
-    @pl.when(b == 1)
-    def _():
-        remote(wk.at[mine], own_slot, pair_s, pair_r, at(sp=partner)).start()
-
-    give = remote(wk.at[mine], own_slot, pair_s, pair_r, at(sp=partner))
+    def give(k, ss, rs):
+        sl = mod(x + k, NX)
+
+        @pl.when(b == 0)
+        def _():
+            remote(wv.at[sl], wbuf.at[p, b, sl], ss, rs, at(sp=partner)).start()
+
+        @pl.when(b == 1)
+        def _():
+            remote(wk.at[sl], wbuf.at[p, b, sl], ss, rs, at(sp=partner)).start()
+
+    give(0, pair_s, pair_r)
 
     items = [mod(p + o, NP) for o in ring_offsets(NP)]
 
@@ -136,9 +150,9 @@
     QN = queries.shape[1] // HEAD
 
     def q_case(j):
-        hl = mod(2 * lax.rem(p, QN // 2) + j, QN)
-        dz = r * (QN // 2) + hl // 2
-        dc = lax.rem(hl, 2)
+        chip, dc = lax.rem(p + j // 2, QN // 2), j % 2
+        hl = 2 * chip + dc
+        dz = r * (QN // 2) + chip
         src = queries.at[:, pl.ds(pl.multiple_of(hl * HEAD, HEAD), HEAD)]
         dst = qbuf.at[pl.ds(pl.multiple_of(z * rows, rows), rows)]
         return src, dst, at(sp=dz, rep=dc), (dz == z) & (dc == r)
@@ -179,14 +193,25 @@
         else:
             acc[...] += d
 
-    pltpu.make_async_copy(wk.at[mine], own_slot, own_s).wait()
-    give.wait_recv()
-    last = NP + XH - 1
+    def first_hops(c):
+        ref = wbuf.at[p, c, x]
+        for d in (0, 1):
+            to = mod(z + 2 if d == 0 else z - 2, NZ)
+            remote(ref, ref, zs, zr.at[d, 0], at(sp=to)).start()
+
+    pltpu.make_async_copy(wk, own_slot, own_s).wait()
+    first_hops(b)
+    drain(wbuf.at[p, 1 - b, x], pair_r)
+    first_hops(1 - b)
+    starts = [None, 1]
+    for i in range(2, NP):
+        starts.append(max((i + 1) // 2, starts[-1] + (i > 2)))
+    last = starts[-1] + XH
     done_dots = 0
+    order = list(range(1, NP)) + [0]
     q_next = 0
-    q_ticks = [0] * (last + 1)
-    for n in range(QN):
-        q_ticks[min(ZH + n // 3, last)] += 1
+    q_ticks = [0] * (ZH - 1) + [2, 2, 3, 3, 3] + [0] * last
+    q_ticks[2 * ZH] = QN - sum(q_ticks)
     for t in range(last + 1):
         with jax.named_scope(f"t{t}"):
             for h in range(XH, 0, -1):
@@ -194,37 +219,44 @@
                     if 1 <= t <= ZH:
                         for d in (0, 1):
                             z_recv(t, d).wait_recv()
-                    if t < ZH:
+                    if 0 < t < ZH:
                         for d in (0, 1):
                             z_send(t + 1, d).start()
-                i = t - (h - 1)
-                if 0 <= i < NP:
-                    for d in (0, 1):
-                        if h > 1:
-                            x_recv(i, h - 1, d).wait_recv()
-                        x_send(i, h, d).start()
+                for i in range(1, NP):
+                    if t == starts[i] + h - 1:
+                        for d in (0, 1):
+                            if h > 1:
+                                x_recv(i, h - 1, d).wait_recv()
+                            x_send(i, h, d).start()
             if t < HC:
                 h_send(t).start()
             if t == 0:
                 pltpu.make_async_copy(hidden, hown, hown_s).wait()
                 norm_into(hown, b * rows)
+            if t in (ZH, ZH + 1):
+                for k in range(1, NX):
+                    if (k <= NX // 2) == (t == ZH):
+                        give(k, rest_s, rest_r)
             for _ in range(q_ticks[t]):
                 start_q(q_next)
                 q_next += 1
             if 3 <= t < HC + 3:
                 h_send(t - 3).wait_recv()
                 h_relay(t - 3).start()
-            if t == HC + 4:
+            if t == HC + 3:
                 drain(hbuf.at[pl.ds(pl.multiple_of((1 - r) * half, half), half)], gr)
                 norm_into(hbuf, (1 - b) * rows)
-            if t >= HC + 4:
+            if t >= HC + 3:
                 for _ in range(2 if t < last else NP):
-                    if done_dots < NP and done_dots + XH <= t:
+                    if done_dots < NP - 1 and starts[order[done_dots]] + XH <= t:
                         for d in (0, 1):
-                            x_recv(done_dots, XH, d).wait_recv()
-                        dot_item(done_dots, done_dots == 0)
+                            x_recv(order[done_dots], XH, d).wait_recv()
+                        dot_item(order[done_dots], done_dots == 0)
                         done_dots += 1
-    assert done_dots == NP and q_next == QN
+            if t == last - 2:
+                drain(wbuf.at[p, 1 - b, pl.ds(0, NX - 1)], rest_r)
+                dot_item(0, False)
+    assert done_dots == NP - 1
 
     NH = kvown.shape[0]
     for j in range(NH):
@@ -232,12 +264,12 @@
 
         @pl.when(b == 0)
         def _():
-            y = acc[:, cols] + bias[0:1, cols]
+            y = acc[:, cols] + kb[cols].astype(F32).reshape(1, HEAD)
             kvown[j] = (y * cos_t[...] + pltpu.roll(y, HEAD // 2, 1) * sin_t[...]).astype(BF16)
 
         @pl.when(b == 1)
         def _():
-            kvown[j] = (acc[:, cols] + bias[1:2, cols]).astype(BF16)
+            kvown[j] = (acc[:, cols] + vb[cols].astype(F32).reshape(1, HEAD)).astype(BF16)
 
     prow = 2 * rows
     span = rows * NZ
@@ -245,9 +277,11 @@
     def unit(a, q):
         return pl.ds(pl.multiple_of((2 - a) * span + q * prow, prow), prow)
 
+    kv_heads = [pick(near_first(NH, NP), mod(p - NH * r, NP), k) for k in range(NH)]
+
     def kv_case(k):
-        j, e = lax.rem(k // 2 + p, NH), k % 2
-        dz = 2 * (NH * r + j) + e
+        j = kv_heads[k]
+        dz = 2 * (NH * r + j) + lax.rem(p, 2)
         return kvown.at[j], buf.at[b, unit(0, p)], at(sp=dz, rep=b), (dz == z) & (b == r)
 
     def start_kv(k):
@@ -261,7 +295,7 @@
         def _():
             remote(src, dst, ks, kr.at[p], dev).start()
 
-    for k in range(2 * NH):
+    for k in range(NH):
         start_kv(k)
 
     def relay(a, q):
@@ -270,20 +304,26 @@
             remote(here, here, ks, kr.at[q], at()).wait_recv()
         else:
             remote(here, here, fs, fr.at[a - 1, q], at()).wait_recv()
+        if a == 0:
+
+            @pl.when(lax.rem(q, 2) == b)
+            def _():
+                remote(here, here, ps, kr.at[q], at(sp=partner)).start()
+
         remote(here, here, ds, dr, at(rep=1 - r)).start()
         if a < 2:
             there = buf.at[r, unit(a + 1, q)]
             remote(here, there, fs, fr.at[a, q], at(blk=mod(x + 1, NX))).start()
 
-    pairs = []
-    for k in range(NH):
-        first = mod(p - k, NH)
-        pairs += [first + NH * c for c in range(NP // NH)]
-    for i in range(NP + 2):
+    for i in range(NP + 4):
         with jax.named_scope(f"relay{i}"):
             for a in (0, 1, 2):
-                if 0 <= i - a < NP:
-                    relay(a, pairs[i - a])
+                if 0 <= i - 2 * a < NP:
+                    relay(a, items[i - 2 * a])
+            if i >= 6 and q_next < QN:
+                start_q(q_next)
+                q_next += 1
+    assert q_next == QN
     with jax.named_scope("relayed"):
         drain(buf.at[1 - r], dr)
         drain(qbuf, qr)
@@ -347,9 +387,10 @@
 
     def q_pair(n, _):
         with jax.named_scope("qtile"):
-            for qi in (n, n + NZ // 2):
+            tiles = (lax.rem(z + NZ // 2 - n + NZ, NZ), lax.rem(z + NZ // 2 + 1 + n, NZ))
+            for qi in tiles:
                 q_tile(qi)
-            for qi in (n, n + NZ // 2):
+            for qi in tiles:
                 send_out(qi)
         return 0
 
@@ -358,12 +399,14 @@
     with jax.named_scope("owait"):
         drain(out, orr)
     with jax.named_scope("sends"):
-        give.wait_send()
+        drain(wbuf.at[p, b, x], pair_s)
+        drain(wbuf.at[p, b, pl.ds(0, NX - 1)], rest_s)
         drain(wbuf.at[pl.ds(0, NP - 1), :, 0], zs)
-        drain(wbuf.at[:, :, pl.ds(0, NX - 1)], xs)
+        drain(wbuf.at[pl.ds(0, NP - 1), :, pl.ds(0, NX - 1)], xs)
         drain(hidden.at[pl.ds(0, half)], hs)
         drain(hidden.at[pl.ds(0, half)], gs)
         drain(buf.at[0], ds)
+        drain(buf.at[0, pl.ds(0, NH * prow)], ps)
         drain(buf.at[0, pl.ds(0, 2 * span)], fs)
 
         q_self = r == z // (NZ // 2)
@@ -377,15 +420,15 @@
             def _():
                 drain(qbuf, sem)
 
-        kv_self = q_self & (b == r)
+        kv_self = q_self & (b == r) & (lax.rem(p, 2) == b)
 
         @pl.when(kv_self)
         def _():
-            drain(buf.at[0, pl.ds(0, (2 * NH - 1) * prow)], ks)
+            drain(buf.at[0, pl.ds(0, (NH - 1) * prow)], ks)
 
         @pl.when(jnp.logical_not(kv_self))
         def _():
-            drain(buf.at[0, pl.ds(0, 2 * NH * prow)], ks)
+            drain(buf.at[0, pl.ds(0, NH * prow)], ks)
 
 
 def on_device(
@@ -406,7 +449,6 @@
     angles = places[:, None] * inverse[None, :]
     cos_t = jnp.cos(angles)
     sin_t = jnp.sin(angles) * jnp.where(lane < HEAD // 2, -1.0, 1.0).astype(F32)
-    bias = jnp.stack([key_shift_bias, value_shift_bias]).astype(F32)
     HC = 4
     QN = queries.shape[2] // HEAD
     dma = pltpu.SemaphoreType.DMA
@@ -415,7 +457,7 @@
     out = pl.pallas_call(
         functools.partial(body, NZ, NX),
         out_shape=jax.ShapeDtypeStruct((rows, queries.shape[2]), BF16),
-        in_specs=[pl.BlockSpec(memory_space=pltpu.SMEM), hbm, hbm, vmem, hbm, hbm] + [vmem] * 3,
+        in_specs=[pl.BlockSpec(memory_space=pltpu.SMEM), hbm, hbm, vmem, hbm, hbm] + [vmem] * 4,
         out_specs=hbm,
         scratch_shapes=[
             pltpu.VMEM((NP, 2, NX, krows // NX, kcols), BF16),
@@ -427,12 +469,12 @@
             pltpu.VMEM((span, HEAD), BF16),
             pltpu.VMEM((2, 3 * span, HEAD), BF16),
             pltpu.VMEM((span, HEAD), BF16),
-            dma(()), dma(()), dma(()), dma(()),
+            dma(()), dma(()), dma(()), dma(()), dma(()), dma(()),
             dma(()), dma((2, NP // 2)),
             dma(()), dma((NP, 2, NX // 2)),
             dma(()), dma((HC,)), dma(()), dma(()),
             dma(()), dma(()),
-            dma(()), dma((NP,)),
+            dma(()), dma((NP,)), dma(()),
             dma(()), dma(()),
             dma(()), dma((2, NP)),
             dma(()), dma(()),
@@ -441,8 +483,9 @@
             collective_id=0, has_side_effects=True, vmem_limit_bytes=56 * 2**20
         ),
     )(
-        doc_lengths, hidden[0], queries[0], norm_gain[None], key_matrix, value_matrix,
-        bias, cos_t, sin_t,
+        doc_lengths, hidden[0], queries[0], norm_gain[None],
+        key_matrix.reshape(NX, krows // NX, kcols), value_matrix.reshape(NX, krows // NX, kcols),
+        key_shift_bias, value_shift_bias, cos_t, sin_t,
     )
     return out[None]
 

time: 182 us -> 175 us (0.962)
  Pallas kernels: 175 us -> 171 us
    pallas_call x1, Pallas kernels: 175 us -> 171 us  [on_device(): pl.pallas_call(functools.partial(body, NZ, NX), out_shape=jax.ShapeDtypeS...]
where the time goes in v3:
time: 175 us
  Pallas kernels  171 us (98%)
  local copies, waits for them, and re-layouts  1.88 us (1%)
    pallas_call x1, Pallas kernels, on_device(): pl.pallas_call(functools.partial(body, NZ, NX), out_shape=jax.ShapeDtypeS...  171 us

profile of v3, /device:TPU:80, one launch (start us, length us, event | category | flops | bytes accessed | tf_op | source)
XLA Modules:
  0.0 174.6 jit_solution(1564988956619143836)
XLA Ops:
  0.0 1.2 fusion
  1.3 171.4 %shard_map.82 = bf16[128,2048]{1,0:T(8,128)(2,1)} custom-call(s32[8]{0:T(128)} %lengths.1, bf16[128,4096]{1,0:T(8,128)(2,1)} %bitcast.7, bf16[128,2048]{1,0:T(8,128)(2,1)} %bitcast.8, f32[1,4096]{1,0:T(1,128)} %bitcast.11, bf16[8,32,512]{2,1,0:T(8,128)(2,1)} %bitcast.9, bf16[8,32,512]{2,1,0:T(8,128)(2,1)} %bitcast.10, bf16[512]{0:T(512)(128)(2,1)} %kb.1, ...), custom_call_target="tpu_custom_call" | custom-call | tf_op jit(solution)/shard_map/pallas_call | solution.py:457
  172.7 1.9 %copy.10 = bf16[1,128,2048]{2,1,0:T(8,128)(2,1)} copy(bf16[1,128,2048]{2,1,0:T(8,128)(2,1)} %bitcast.6) | data formatting | bytes 1048576
  (2 shorter events, 0.0 us)

commit v4 on v3

--- a/solution.py
+++ b/solution.py
@@ -304,22 +304,36 @@
             remote(here, here, ks, kr.at[q], at()).wait_recv()
         else:
             remote(here, here, fs, fr.at[a - 1, q], at()).wait_recv()
-        if a == 0:
-
-            @pl.when(lax.rem(q, 2) == b)
+        came_here = lax.rem(q, 2) == b
+        if a != 1:
+
+            @pl.when(came_here)
             def _():
-                remote(here, here, ps, kr.at[q], at(sp=partner)).start()
+                remote(here, here, ps, kr.at[q] if a == 0 else fr.at[1, q], at(sp=partner)).start()
 
         remote(here, here, ds, dr, at(rep=1 - r)).start()
         if a < 2:
-            there = buf.at[r, unit(a + 1, q)]
-            remote(here, there, fs, fr.at[a, q], at(blk=mod(x + 1, NX))).start()
-
+
+            @pl.when(came_here | (a == 0))
+            def _():
+                there = buf.at[r, unit(a + 1, q)]
+                remote(here, there, fs, fr.at[a, q], at(blk=mod(x + 1, NX))).start()
+
+    offs = ring_offsets(NP)
+    split = [[o for o in offs if o % 2 == parity] for parity in (0, 1)]
+    orders = []
+    for here, other in (split, split[::-1]):
+        order = here[:1]
+        for k in range(1, len(here)):
+            order += [here[k], other[k - 1]]
+        orders.append(order + other[-1:])
+    same = b == lax.rem(p, 2)
+    pairs = [mod(p + jnp.where(same, o, e), NP) for o, e in zip(*orders)]
     for i in range(NP + 4):
         with jax.named_scope(f"relay{i}"):
             for a in (0, 1, 2):
                 if 0 <= i - 2 * a < NP:
-                    relay(a, items[i - 2 * a])
+                    relay(a, pairs[i - 2 * a])
             if i >= 6 and q_next < QN:
                 start_q(q_next)
                 q_next += 1
@@ -406,8 +420,8 @@
         drain(hidden.at[pl.ds(0, half)], hs)
         drain(hidden.at[pl.ds(0, half)], gs)
         drain(buf.at[0], ds)
-        drain(buf.at[0, pl.ds(0, NH * prow)], ps)
-        drain(buf.at[0, pl.ds(0, 2 * span)], fs)
+        drain(buf.at[0, pl.ds(0, 2 * NH * prow)], ps)
+        drain(buf.at[0, pl.ds(0, span + NH * prow)], fs)
 
         q_self = r == z // (NZ // 2)
         for sem in (qs, os):

time: 175 us -> 167 us (0.954)
  Pallas kernels: 171 us -> 164 us
    pallas_call x1, Pallas kernels: 171 us -> 164 us  [on_device(): pl.pallas_call(functools.partial(body, NZ, NX), out_shape=jax.ShapeDtypeS...]
where the time goes in v4:
time: 167 us
  Pallas kernels  164 us (98%)
  local copies, waits for them, and re-layouts  1.88 us (1%)
    pallas_call x1, Pallas kernels, on_device(): pl.pallas_call(functools.partial(body, NZ, NX), out_shape=jax.ShapeDtypeS...  164 us

profile of v4, /device:TPU:80, one launch (start us, length us, event | category | flops | bytes accessed | tf_op | source)
XLA Modules:
  0.0 166.8 jit_solution(14443126533696435789)
XLA Ops:
  0.0 1.2 fusion
  1.3 163.6 %shard_map.82 = bf16[128,2048]{1,0:T(8,128)(2,1)} custom-call(s32[8]{0:T(128)} %lengths.1, bf16[128,4096]{1,0:T(8,128)(2,1)} %bitcast.7, bf16[128,2048]{1,0:T(8,128)(2,1)} %bitcast.8, f32[1,4096]{1,0:T(1,128)} %bitcast.11, bf16[8,32,512]{2,1,0:T(8,128)(2,1)} %bitcast.9, bf16[8,32,512]{2,1,0:T(8,128)(2,1)} %bitcast.10, bf16[512]{0:T(512)(128)(2,1)} %kb.1, ...), custom_call_target="tpu_custom_call" | custom-call | tf_op jit(solution)/shard_map/pallas_call | solution.py:471
  164.9 1.9 %copy.10 = bf16[1,128,2048]{2,1,0:T(8,128)(2,1)} copy(bf16[1,128,2048]{2,1,0:T(8,128)(2,1)} %bitcast.6) | data formatting | bytes 1048576
  (2 shorter events, 0.0 us)
